TPU v7x, 32 devices: a whole 2x2x4 slice. The times are simulated.
32 devices in a mesh: grp: 4 (over z), cand: 8 (over y, x, core).
Axes of the slice: x: 2, y: 2, z: 4, core: 2. Of those that a mesh axis runs over, the one named last changes fastest.
Arguments:
- embeddings: bfloat16 [96, 1024, 1024], P('grp', 'cand'), may hold values from -6 to 6
- hidden_weight: bfloat16 [2048, 1024], P('cand'), may hold values from -0.1875 to 0.1875
- score_weight: bfloat16 [2048], replicated, may hold values from -0.5 to 0.5
- relevance: int32 [96, 1024], P('grp', 'cand'), may hold values from 0 to 4
- rank_pos: int32 [96, 1024], P('grp', 'cand'), may hold values from 0 to 1023, as said below
- ideal_dcg: float32 [96], P('grp'), may hold values from 32 to 128
Outputs:
- grad_hidden: float32 [2048, 1024], P('cand')
- lambdas: float32 [96, 1024], P('grp', 'cand')
Inputs may be any that keep to these rules, and one draw needn't show every extreme that they name: `rank_pos`: in each group the rank positions are a permutation of 0 to 1023.
All inputs are finite; a program needn't handle non-finite values.
Results may differ from a plain program's by a relative error of at most 0.006.
Values may be sent and summed in bfloat16 or wider, within the bound.
A program may use at most 64 MiB of HBM per device.

v0:
```python
import jax
import jax.numpy as jnp
from jax import lax
from jax.sharding import PartitionSpec as P

EPS = 1e-06


def pair_lambdas(own_score, own_gain, own_disc, far_score, far_gain, far_disc, ideal):
    gain_diff = far_gain[..., None, :] - own_gain[..., :, None]
    toward = jnp.sign(gain_diff)
    weight = (
        jnp.abs(gain_diff)
        * jnp.abs(far_disc[..., None, :] - own_disc[..., :, None])
        / ideal[..., None, None]
    )
    margin = own_score[..., :, None] - far_score[..., None, :]
    return jnp.sum(weight * toward * jax.nn.sigmoid(toward * margin), axis=-1)


def gain_of(labels):
    return jnp.exp2(labels.astype(jnp.float32)) - 1.0


def discount_of(positions):
    return 1.0 / jnp.log2(2.0 + positions.astype(jnp.float32))


def per_device(embeddings, hidden_weight, score_weight, relevance, rank_pos, ideal_dcg):
    grp_count, local, width = embeddings.shape
    cand_rows = embeddings.reshape(grp_count * local, width)
    pre_act = lax.dot_general(
        cand_rows,
        lax.all_gather(hidden_weight, "cand", axis=0, tiled=True),
        (((1,), (1,)), ((), ())),
        preferred_element_type=jnp.float32,
    )
    acts, pull = jax.vjp(jax.nn.gelu, pre_act)
    scores = jnp.dot(
        acts.astype(jnp.bfloat16), score_weight, preferred_element_type=jnp.float32
    ).reshape(grp_count, local)
    gain_vals = gain_of(relevance)
    discount = discount_of(rank_pos)
    lambdas = pair_lambdas(
        scores,
        gain_vals,
        discount,
        lax.all_gather(scores, "cand", axis=1, tiled=True),
        lax.all_gather(gain_vals, "cand", axis=1, tiled=True),
        lax.all_gather(discount, "cand", axis=1, tiled=True),
        ideal_dcg,
    )
    upstream = (
        lambdas.reshape(grp_count * local)[:, None] * score_weight.astype(jnp.float32)[None, :]
    )
    grad_pre = pull(upstream)[0].astype(jnp.bfloat16)
    owned = lax.psum_scatter(
        lax.dot_general(
            grad_pre, cand_rows, (((0,), (0,)), ((), ())), preferred_element_type=jnp.float32
        ).astype(jnp.bfloat16),
        "cand",
        scatter_dimension=0,
        tiled=True,
    ).astype(jnp.float32)
    summed = lax.psum(owned, "grp")
    squares = lax.psum(jnp.sum(summed * summed), "cand")
    entries = summed.shape[0] * summed.shape[1] * lax.axis_size("cand")
    scale = lax.rsqrt(squares / entries + EPS)
    return (summed * scale, lambdas)


def solution(mesh):
    return jax.shard_map(
        per_device,
        mesh=mesh,
        in_specs=(
            P("grp", "cand", None),
            P("cand", None),
            P(),
            P("grp", "cand"),
            P("grp", "cand"),
            P("grp"),
        ),
        out_specs=(P("cand", None), P("grp", "cand")),
        check_vma=False,
    )
```

profile of v0, /device:TPU:0, one launch (start us, length us, event | category | flops | bytes accessed | tf_op | source)
XLA Modules:
  0.0 254.7 jit_solution(1957202030902142692)
XLA Ops:
  7.2 0.0 all-gather.2.cloned.1.call-start
  7.2 0.7 all-gather.2.cloned.1.call-update
  7.9 0.0 reduce-scatter.2.cloned.1.call-start
  7.9 0.7 reshape.18
  8.6 0.7 convert_element_type.24
  9.3 0.7 exponential_add_fusion
  10.0 10.7 %all_gather.12 = f32[24,1024]{1,0:T(8,128)S(1)} all-gather(f32[24,128]{1,0:T(8,128)S(1)} %exponential_add_fusion), channel_id=1, replica_groups=mesh['grp'=4,'cand'=8] {'cand'}, dimensions={1}, use_global_device_ids=true | all-gather | bytes 110592 | tf_op jit(solution)/shard_map/all_gather | solution.py:49
  20.7 0.7 multiply_divide_fusion
  21.5 9.5 %all_gather.13 = f32[24,1024]{1,0:T(8,128)S(1)} all-gather(f32[24,128]{1,0:T(8,128)S(1)} %multiply_divide_fusion), channel_id=1, replica_groups=mesh['grp'=4,'cand'=8] {'cand'}, dimensions={1}, use_global_device_ids=true | all-gather | bytes 110592 | tf_op jit(solution)/shard_map/all_gather | solution.py:50
  31.0 18.5 %all-gather.2.cloned.1.call-done = bf16[2048,1024]{1,0:T(8,128)(2,1)} async-done(((bf16[256,1024]{1,0:T(8,128)(2,1)}), bf16[2048,1024]{1,0:T(8,128)(2,1)}) %all-gather.2.cloned.1.call-update) | async-done | bytes 4194320 | tf_op jit(solution)/shard_map/all_gather | solution.py:34
  49.5 19.7 %fusion.36 = f32[3072,2048]{1,0:T(8,128)} fusion(bf16[3072,1024]{1,0:T(8,128)(2,1)} %bitcast.11, bf16[2048,1024]{1,0:T(8,128)(2,1)} %all-gather.2.cloned.1.call-done), kind=kOutput, calls=%fused_computation.44 | convolution fusion | flops 12884901888 | bytes 35651584 | tf_op jit(solution)/shard_map/dot_general | solution.py:32
  69.1 0.0 copy-start
  69.1 11.9 %fusion.20 = f32[1,3072]{1,0:T(1,128)S(1)} fusion(bf16[2048,1]{0,1:T(2,128)(2,1)S(1)} %reshape.18, f32[3072,2048]{1,0:T(8,128)} %fusion.36), kind=kOutput, calls=%fused_computation.27 | convolution fusion | flops 69206016 | bytes 25182208 | tf_op jit(solution)/shard_map/dot_general | solution.py:39
  81.1 9.1 %all_gather.15 = f32[24,1024]{1,0:T(8,128)S(1)} all-gather(f32[24,128]{1,0:T(8,128)S(1)} %bitcast.9), channel_id=1, replica_groups=mesh['grp'=4,'cand'=8] {'cand'}, dimensions={1}, use_global_device_ids=true | all-gather | bytes 110592 | tf_op jit(solution)/shard_map/all_gather | solution.py:48
  90.2 0.0 copy-done
  90.2 11.2 %fusion.13 = f32[24,128]{1,0:T(8,128)S(1)} fusion(f32[24,1024]{1,0:T(8,128)S(1)} %all_gather.15, f32[24,128]{1,0:T(8,128)S(1)} %bitcast.10, f32[24]{0:T(128)S(1)} %copy-done, f32[24,128]{1,0:T(8,128)S(1)} %multiply_divide_fusion, f32[24,1024]{1,0:T(8,128)S(1)} %all_gather.13, f32[24,128]{1,0:T(8,128)S(1)} %exponential_add_fusion, f32[24,1024]{1,0:T(8,128)S(1)} %all_gather.12), kind=kLoop, calls=%fused_computation.20 | loop fusion | flops 47182848 | bytes 344160 | tf_op jit(solution)/shard_map/reduce_sum | solution.py:18
  101.4 0.0 copy-start.1
  101.4 35.9 %fusion.23 = bf16[2048,1024]{1,0:T(8,128)(2,1)} fusion(bf16[3072,1024]{1,0:T(8,128)(2,1)} %bitcast.12, f32[3072,2048]{1,0:T(8,128)} %fusion.36, f32[2048]{0:T(1024)S(1)} %convert_element_type.24, f32[3072]{0:T(1024)S(1)} %bitcast.13), kind=kOutput, calls=%fused_computation.29 | convolution fusion | flops 13019119616 | bytes 35672064 | tf_op jit(solution)/shard_map/dot_general | solution.py:58
  137.3 0.0 copy-done.1
  137.3 0.0 reduce-scatter.2.cloned.1.call-update
  137.4 51.3 %reduce-scatter.2.cloned.1.call-done = bf16[256,1024]{1,0:T(8,128)(2,1)} async-done(((bf16[2048,1024]{1,0:T(8,128)(2,1)}), bf16[256,1024]{1,0:T(8,128)(2,1)}) %reduce-scatter.2.cloned.1.call-update) | async-done | bytes 524304 | tf_op jit(solution)/shard_map/reduce_scatter | solution.py:57
  188.7 44.2 %all-reduce.1 = f32[256,1024]{1,0:T(8,128)S(1)} all-reduce(bf16[256,1024]{1,0:T(8,128)(2,1)} %reduce-scatter.2.cloned.1.call-done), channel_id=1, replica_groups=mesh['grp'=4,'cand'=8] {'grp'}, use_global_device_ids=true, to_apply=%region_2.0 | all-reduce | flops 262144 | bytes 1572864 | tf_op jit(solution)/shard_map/psum | solution.py:65
  232.9 0.9 multiply_reduce_fusion
  233.8 12.4 %psum.15 = f32[]{:T(128)} all-reduce(f32[]{:T(128)} %multiply_reduce_fusion), channel_id=1, replica_groups=mesh['grp'=4,'cand'=8] {'cand'}, use_global_device_ids=true, to_apply=%region_4.0 | all-reduce | flops 1 | bytes 8 | tf_op jit(solution)/shard_map/psum | solution.py:66
  246.9 1.0 broadcast_multiply_fusion
Async XLA Ops:
  7.2 42.3 %all-gather.2.cloned.1.call-start = ((), (), s32[]{:S(2)}) async-start(), calls=%async_computation.1 | async-start | bytes 4718592 | tf_op jit(solution)/shard_map/all_gather | solution.py:34
  7.9 180.8 %reduce-scatter.2.cloned.1.call-start = ((), (), s32[]{:S(2)}) async-start(), calls=%async_computation.2 | async-start | bytes 4718592 | tf_op jit(solution)/shard_map/reduce_scatter | solution.py:57
  69.1 21.1 %copy-start = (f32[24]{0:T(128)S(1)}, f32[24]{0:T(128)}, u32[]{:S(2)}) copy-start(f32[24]{0:T(128)} %param.11) | copy-start | bytes 292
  101.4 36.0 %copy-start.1 = (f32[24,128]{1,0:T(8,128)}, f32[24,128]{1,0:T(8,128)S(1)}, u32[]{:S(2)}) copy-start(f32[24,128]{1,0:T(8,128)S(1)} %fusion.13) | copy-start | bytes 36868
Sparse Core Ops, SparseCore 0:
  9.9 39.5 all-gather.1
  137.5 51.1 reduce-scatter.1
where the time goes:
time: 255 us
  blocking collectives  86 us (34%)
  waiting for transfers between devices  70.5 us (28%)
  matrix products  67.5 us (26%)
  other arithmetic  15.2 us (6%)
  between operations  14.8 us (6%)
    reduce_scatter x1, waiting for transfers between devices, per_device(): lax.psum_scatter(lax.dot_general(grad_pre, cand_rows, (((0,), (0,)), ((),...  51.3 us
    psum x1, blocking collectives, per_device(): summed = lax.psum(owned, 'grp')  44.2 us
    dot_general x1, matrix products, per_device(): lax.dot_general(grad_pre, cand_rows, (((0,), (0,)), ((), ())), preferred_...  35.9 us
    dot_general x1, matrix products, per_device(): lax.dot_general(cand_rows, lax.all_gather(hidden_weight, 'cand', axis=0,...  19.7 us
    all_gather x1, waiting for transfers between devices, per_device(): lax.all_gather(hidden_weight, 'cand', axis=0, tiled=True)  18.5 us
    psum x1, blocking collectives, per_device(): squares = lax.psum(jnp.sum(summed * summed), 'cand')  12.4 us
    dot_general x1, matrix products, per_device(): jnp.dot(acts.astype(jnp.bfloat16), score_weight, preferred_element_type=j...  11.9 us
    reduce_sum x1, other arithmetic, pair_lambdas(): return jnp.sum(weight * toward * jax.nn.sigmoid(toward * margin), axis=-1)  11.2 us
  transfers between devices with their start and end apart: 2, of which 2 were waited for; matrix products, arithmetic and copies ran while one was open for 1% of the time, Pallas kernels for 0%

commit v1 on v0

--- a/solution.py
+++ b/solution.py
@@ -1,6 +1,10 @@
+import functools
+
 import jax
 import jax.numpy as jnp
 from jax import lax
+from jax.experimental import pallas as pl
+from jax.experimental.pallas import tpu as pltpu
 from jax.sharding import PartitionSpec as P
 
 EPS = 1e-06
@@ -26,7 +30,7 @@
     return 1.0 / jnp.log2(2.0 + positions.astype(jnp.float32))
 
 
-def per_device(embeddings, hidden_weight, score_weight, relevance, rank_pos, ideal_dcg):
+def per_device_plain(embeddings, hidden_weight, score_weight, relevance, rank_pos, ideal_dcg):
     grp_count, local, width = embeddings.shape
     cand_rows = embeddings.reshape(grp_count * local, width)
     pre_act = lax.dot_general(
@@ -69,9 +73,456 @@
     return (summed * scale, lambdas)
 
 
+MESH = pl.DeviceIdType.MESH
+GELU_C = 0.7978845608028654
+GELU_A = 0.044715
+PLANE = 8
+LANES = 128
+W_DIRECT = [(0, 0, 1), (0, 1, 1), (0, 0, 4), (0, 1, 2), (0, 0, 2), (0, 1, 4)]
+
+
+def step_kernel(
+    groups,
+    emb_hbm,
+    w_hbm,
+    sw_ref,
+    gd_ref,
+    hinv_ref,
+    tot_ref,
+    sq_ref,
+    lam_ref,
+    emb,
+    wall,
+    dpre,
+    gbuf,
+    scacc,
+    all_s,
+    all_gd,
+    cols,
+    lam_t,
+    lrow,
+    p_send,
+    p_recv,
+    s6,
+    s2,
+    s4,
+    t32,
+    x4,
+    y2,
+    x0,
+    y0,
+    zs,
+    zr,
+    sq_all,
+    loc_sem,
+    w_ss,
+    w_rs,
+    g_ss,
+    g_rs,
+    s_ss,
+    s_rs,
+    p_ss,
+    p_rs,
+    a_ss,
+    a_rs,
+    z_ss,
+    z_rs,
+    q_ss,
+    q_rs,
+):
+    c = lax.axis_index("cand")
+    z = lax.axis_index("grp")
+    n_z = zr.shape[0] + 1
+    hs = wall.shape[1]
+    half = hs // 2
+    rows, width = emb.shape
+
+    def flip(value, mask):
+        out, bit = 0, 1
+        while bit < PLANE:
+            b = (value // bit) % 2
+            out = out + bit * ((1 - b) if mask & bit else b)
+            bit *= 2
+        return out
+
+    def zflip(mask):
+        out, bit = 0, 1
+        while bit < n_z:
+            b = (z // bit) % 2
+            out = out + bit * ((1 - b) if mask & bit else b)
+            bit *= 2
+        return out
+
+    def to(r):
+        return {"cand": flip(c, r)}
+
+    def tz(q):
+        return {"grp": zflip(q)}
+
+    def remote(src, dst, ss, rs, dev):
+        return pltpu.make_async_remote_copy(
+            src_ref=src, dst_ref=dst, send_sem=ss, recv_sem=rs, device_id=dev, device_id_type=MESH
+        )
+
+    w_in = pltpu.make_async_copy(w_hbm, wall.at[0], loc_sem.at[0])
+    e_in = pltpu.make_async_copy(emb_hbm, emb, loc_sem.at[1])
+    g_in = pltpu.make_async_copy(gd_ref, all_gd.at[0], loc_sem.at[2])
+    w_in.start()
+    g_in.start()
+    e_in.start()
+
+    barrier = pltpu.get_barrier_semaphore()
+    for r in range(1, PLANE):
+        pl.semaphore_signal(barrier, inc=1, device_id=to(r), device_id_type=MESH)
+    for q in range(1, n_z):
+        pl.semaphore_signal(barrier, inc=1, device_id=tz(q), device_id_type=MESH)
+    pl.semaphore_wait(barrier, PLANE - 1 + n_z - 1)
+
+    def w_copy(src, h, hop):
+        dst = src ^ hop
+        part = pl.ds(h * half, half)
+        return remote(
+            wall.at[src, part], wall.at[dst, part], w_ss.at[dst, h], w_rs.at[dst, h], to(hop)
+        )
+
+    started = []
+
+    def go(copy):
+        copy.start()
+        started.append(copy)
+        return copy
+
+    w_in.wait()
+    by_dst = {}
+    for src, h, hop in W_DIRECT:
+        by_dst[src ^ hop, h] = go(w_copy(src, h, hop))
+    g_in.wait()
+    gd_copies = [
+        go(remote(all_gd.at[0], all_gd.at[r], g_ss.at[r - 1], g_rs.at[r - 1], to(r)))
+        for r in range(1, PLANE)
+    ]
+    e_in.wait()
+
+    scacc[...] = jnp.zeros_like(scacc)
+    tile = 2 * LANES
+    inner = 3 if rows % (3 * tile) == 0 else 1
+
+    def forward_block(r):
+        blk = pl.multiple_of(flip(c, r) * hs, hs)
+        sw = sw_ref[pl.ds(blk, hs), :]
+
+        @pl.loop(0, rows // (tile * inner))
+        def _(step):
+            for u in range(inner):
+                at = pl.multiple_of((step * inner + u) * tile, tile)
+                x = lax.dot_general(
+                    wall[r],
+                    emb[pl.ds(at, tile), :],
+                    (((1,), (1,)), ((), ())),
+                    preferred_element_type=jnp.float32,
+                )
+                x2 = x * x
+                t = jnp.tanh(x * (GELU_C + (GELU_C * GELU_A) * x2))
+                h = 0.5 + 0.5 * t
+                act = x * h
+                slope = h + act * ((1.0 - h) * (2 * GELU_C + (6 * GELU_C * GELU_A) * x2))
+                dpre[r, :, pl.ds(at, tile)] = slope * sw
+                scacc[:, pl.ds(at, tile)] += jnp.sum(
+                    (act * sw).reshape(hs // 8, 8, tile), axis=0
+                )
+
+    def arrived(r, h):
+        by_dst[r, h].wait_recv()
+
+    def pass_on(src, h, hop):
+        by_dst[src ^ hop, h] = go(w_copy(src, h, hop))
+
+    forward_block(0)
+    arrived(1, 0)
+    arrived(1, 1)
+    forward_block(1)
+    arrived(4, 0)
+    pass_on(4, 0, 2)
+    pass_on(4, 0, 1)
+    arrived(2, 1)
+    pass_on(2, 1, 4)
+    pass_on(2, 1, 1)
+    arrived(2, 0)
+    pass_on(2, 0, 1)
+    arrived(4, 1)
+    pass_on(4, 1, 1)
+    forward_block(2)
+    forward_block(4)
+    arrived(3, 0)
+    arrived(3, 1)
+    forward_block(3)
+    arrived(6, 0)
+    pass_on(6, 0, 1)
+    arrived(6, 1)
+    pass_on(6, 1, 1)
+    arrived(5, 0)
+    arrived(5, 1)
+    forward_block(5)
+    forward_block(6)
+    arrived(7, 0)
+    arrived(7, 1)
+    forward_block(7)
+
+    score_row = 0.5 * jnp.sum(scacc[...], axis=0, keepdims=True)
+    for g in range(groups):
+        all_s[0, g : g + 1, :] = score_row[:, g * LANES : (g + 1) * LANES]
+    s_copies = [
+        go(remote(all_s.at[0], all_s.at[r], s_ss.at[r - 1], s_rs.at[r - 1], to(r)))
+        for r in range(1, PLANE)
+    ]
+
+    fill = jnp.zeros((LANES - groups, LANES), jnp.float32)
+
+    def turned(value):
+        return jnp.transpose(jnp.concatenate([value, fill], axis=0))
+
+    cols[0] = turned(all_s[0])
+    cols[1] = turned(all_gd[0, 0])
+    cols[2] = turned(all_gd[0, 1])
+    for copy in gd_copies:
+        copy.wait_recv()
+    for copy in s_copies:
+        copy.wait_recv()
+
+    lam_t[...] = jnp.zeros_like(lam_t)
+    for g in range(groups):
+        si = jnp.broadcast_to(cols[0, :, g : g + 1], (LANES, LANES))
+        gi = jnp.broadcast_to(cols[1, :, g : g + 1], (LANES, LANES))
+        di = jnp.broadcast_to(cols[2, :, g : g + 1], (LANES, LANES))
+        acc = jnp.zeros((LANES, LANES), jnp.float32)
+        for r in range(PLANE):
+            gain_diff = all_gd[r, 0, g : g + 1, :] - gi
+            far = jnp.abs(all_gd[r, 1, g : g + 1, :] - di)
+            t = jnp.tanh(si - all_s[r, g : g + 1, :])
+            acc = acc + far * (gain_diff + jnp.abs(gain_diff) * t)
+        lam_t[:, g : g + 1] = jnp.sum(acc, axis=1, keepdims=True)
+    lam = jnp.transpose(lam_t[...])[:groups, :] * hinv_ref[...]
+    lam_ref[...] = lam
+    for g in range(groups):
+        lrow[:, g * LANES : (g + 1) * LANES] = lam[g : g + 1, :]
+
+    ntile = 2 * LANES
+
+    def grad_block(r, finish):
+        @pl.loop(0, rows // (2 * tile))
+        def _(step):
+            at = pl.multiple_of(step * 2 * tile, 2 * tile)
+            part = pl.ds(at, 2 * tile)
+            gbuf[:, part] = (dpre[r, :, part] * lrow[:, part]).astype(jnp.bfloat16)
+
+        @pl.loop(0, width // ntile)
+        def _(step):
+            at = pl.multiple_of(step * ntile, ntile)
+            part = pl.ds(at, ntile)
+            finish(
+                part,
+                jnp.dot(gbuf[...], emb[:, part], preferred_element_type=jnp.float32),
+            )
+
+    def odd(r):
+        slot = r // 2
+
+        def finish(part, value):
+            p_send[slot, :, part] = value.astype(jnp.bfloat16)
+
+        grad_block(r, finish)
+        return go(remote(p_send.at[slot], p_recv.at[slot], p_ss.at[slot], p_rs.at[slot], to(1)))
+
+    def even(r, copy, out):
+        def finish(part, value):
+            out[:, part] = value.astype(out.dtype)
+
+        grad_block(r, finish)
+        copy.wait_recv()
+
+    def chip_sum(r, copy, out):
+        even(r, copy, t32)
+        out_value = t32[...] + p_recv[r // 2].astype(jnp.float32)
+        if out is None:
+            t32[...] = out_value
+        else:
+            out[...] = out_value.astype(out.dtype)
+
+    low, high = pl.ds(0, half), pl.ds(half, half)
+
+    def axis_copy(i, src, dst, hop):
+        return go(remote(src, dst, a_ss.at[i], a_rs.at[i], to(hop)))
+
+    copy = odd(7)
+    chip_sum(6, copy, s6)
+    to_x4 = axis_copy(0, s6.at[low], x4, 2)
+    to_y2 = axis_copy(1, s6.at[high], y2, 4)
+    copy = odd(3)
+    chip_sum(2, copy, None)
+    s2[low, :] = t32[low, :].astype(jnp.bfloat16)
+    x0_low = axis_copy(2, s2.at[low], x0.at[low], 2)
+    zs[...] = t32[...]
+    copy = odd(5)
+    to_y2.wait_recv()
+    s2[high, :] = (zs[high, :] + y2[...].astype(jnp.float32)).astype(jnp.bfloat16)
+    x0_high = axis_copy(3, s2.at[high], x0.at[high], 2)
+    chip_sum(4, copy, None)
+    s4[high, :] = t32[high, :].astype(jnp.bfloat16)
+    y0_high = axis_copy(4, s4.at[high], y0.at[high], 4)
+    to_x4.wait_recv()
+    s4[low, :] = (t32[low, :] + x4[...].astype(jnp.float32)).astype(jnp.bfloat16)
+    y0_low = axis_copy(5, s4.at[low], y0.at[low], 4)
+    copy = odd(1)
+    chip_sum(0, copy, None)
+    for copy in (x0_low, y0_high, x0_high, y0_low):
+        copy.wait_recv()
+    t32[...] = t32[...] + x0[...].astype(jnp.float32) + y0[...].astype(jnp.float32)
+
+    zpart = hs // n_z
+    s6_done, s6_done2 = to_x4, to_y2
+    s6_done.wait_send()
+    s6_done2.wait_send()
+    s6[...] = t32[...].astype(jnp.bfloat16)
+
+    def zrows(index):
+        return pl.ds(pl.multiple_of(index * zpart, zpart), zpart)
+
+    z_copies = [
+        go(remote(s6.at[zrows(zflip(q))], zr.at[q - 1], z_ss.at[q - 1], z_rs.at[q - 1], tz(q)))
+        for q in range(1, n_z)
+    ]
+    part = t32[zrows(z), :]
+    for q, copy in enumerate(z_copies):
+        copy.wait_recv()
+        part = part + zr[q].astype(jnp.float32)
+    tot_ref[zrows(z), :] = part.astype(jnp.bfloat16)
+    out_copies = [
+        go(
+            remote(
+                tot_ref.at[zrows(z)],
+                tot_ref.at[zrows(z)],
+                z_ss.at[n_z - 2 + q],
+                z_rs.at[n_z - 2 + q],
+                tz(q),
+            )
+        )
+        for q in range(1, n_z)
+    ]
+    for copy in out_copies:
+        copy.wait_recv()
+    total = tot_ref[...].astype(jnp.float32)
+    sq_all[0] = jnp.sum((total * total).reshape(hs // 8, 8, width), axis=0).reshape(
+        8, width // LANES, LANES
+    ).sum(axis=1)
+    q_copies = [
+        go(remote(sq_all.at[0], sq_all.at[r], q_ss.at[r - 1], q_rs.at[r - 1], to(r)))
+        for r in range(1, PLANE)
+    ]
+    for copy in q_copies:
+        copy.wait_recv()
+    sq_ref[...] = jnp.sum(sq_all[...], axis=0)
+    done = (to_x4, to_y2)
+    for copy in started:
+        if copy is not done[0] and copy is not done[1]:
+            copy.wait_send()
+
+
+def per_device_fused(embeddings, hidden_weight, score_weight, relevance, rank_pos, ideal_dcg):
+    groups, local, width = embeddings.shape
+    rows = groups * local
+    hs = hidden_weight.shape[0]
+    hidden = score_weight.shape[0]
+    n_z = lax.axis_size("grp")
+    gain_disc = jnp.stack([gain_of(relevance), discount_of(rank_pos)])
+    hinv = jnp.broadcast_to((0.5 / ideal_dcg)[:, None], (groups, local))
+    bf, f32 = jnp.bfloat16, jnp.float32
+    vmem = pl.BlockSpec(memory_space=pltpu.VMEM)
+    hbm = pl.BlockSpec(memory_space=pl.ANY)
+    dma = pltpu.SemaphoreType.DMA
+    half = hs // 2
+    total, squares, lambdas = pl.pallas_call(
+        functools.partial(step_kernel, groups),
+        out_shape=(
+            jax.ShapeDtypeStruct((hs, width), bf),
+            jax.ShapeDtypeStruct((8, LANES), f32),
+            jax.ShapeDtypeStruct((groups, local), f32),
+        ),
+        in_specs=[hbm, hbm, vmem, hbm, vmem],
+        out_specs=(vmem, vmem, vmem),
+        scratch_shapes=[
+            pltpu.VMEM((rows, width), bf),
+            pltpu.VMEM((PLANE, hs, width), bf),
+            pltpu.VMEM((PLANE, hs, rows), f32),
+            pltpu.VMEM((hs, rows), bf),
+            pltpu.VMEM((8, rows), f32),
+            pltpu.VMEM((PLANE, groups, local), f32),
+            pltpu.VMEM((PLANE, 2, groups, local), f32),
+            pltpu.VMEM((3, LANES, LANES), f32),
+            pltpu.VMEM((LANES, LANES), f32),
+            pltpu.VMEM((1, rows), f32),
+            pltpu.VMEM((PLANE // 2, hs, width), bf),
+            pltpu.VMEM((PLANE // 2, hs, width), bf),
+            pltpu.VMEM((hs, width), bf),
+            pltpu.VMEM((hs, width), bf),
+            pltpu.VMEM((hs, width), bf),
+            pltpu.VMEM((hs, width), f32),
+            pltpu.VMEM((half, width), bf),
+            pltpu.VMEM((half, width), bf),
+            pltpu.VMEM((hs, width), bf),
+            pltpu.VMEM((hs, width), bf),
+            pltpu.VMEM((hs, width), f32),
+            pltpu.VMEM((n_z - 1, hs // n_z, width), bf),
+            pltpu.VMEM((PLANE, 8, LANES), f32),
+            dma((3,)),
+            dma((PLANE, 2)),
+            dma((PLANE, 2)),
+            dma((PLANE - 1,)),
+            dma((PLANE - 1,)),
+            dma((PLANE - 1,)),
+            dma((PLANE - 1,)),
+            dma((PLANE // 2,)),
+            dma((PLANE // 2,)),
+            dma((6,)),
+            dma((6,)),
+            dma((2 * (n_z - 1),)),
+            dma((2 * (n_z - 1),)),
+            dma((PLANE - 1,)),
+            dma((PLANE - 1,)),
+        ],
+        compiler_params=pltpu.CompilerParams(
+            collective_id=0, has_side_effects=True, vmem_limit_bytes=64000 * 1024
+        ),
+    )(
+        embeddings.reshape(rows, width),
+        hidden_weight,
+        score_weight.astype(f32).reshape(hidden, 1),
+        gain_disc,
+        hinv,
+    )
+    scale = lax.rsqrt(jnp.sum(squares) / (hidden * width) + EPS)
+    return (total.astype(f32) * scale, lambdas)
+
+
+def choose(embeddings, hidden_weight, *rest):
+    groups, local, width = embeddings.shape
+    n_z = lax.axis_size("grp")
+    fits = (
+        lax.axis_size("cand") == PLANE
+        and local == LANES
+        and groups <= LANES
+        and (groups * local) % (4 * LANES) == 0
+        and width % (2 * LANES) == 0
+        and n_z > 1
+        and n_z & (n_z - 1) == 0
+        and hidden_weight.shape[0] % (16 * n_z) == 0
+    )
+    body = per_device_fused if fits else per_device_plain
+    return body(embeddings, hidden_weight, *rest)
+
+
 def solution(mesh):
     return jax.shard_map(
-        per_device,
+        choose,
         mesh=mesh,
         in_specs=(
             P("grp", "cand", None),

time: 255 us -> 123 us (0.48)
  Pallas kernels: 0 us -> 112 us
  blocking collectives: 86 us -> 0 us
  waiting for transfers between devices: 70.5 us -> 0 us
  matrix products: 67.5 us -> 0 us
  between operations: 14.8 us -> 1.34 us
  other arithmetic: 15.2 us -> 6.11 us
  local copies, waits for them, and re-layouts: 0.71 us -> 3.32 us
    pallas_call x0 -> x1, Pallas kernels: none -> 112 us  [per_device_fused(): pl.pallas_call(functools.partial(step_kernel, groups), out_shape=(jax.Sha...]
    dot_general x3 -> x0, matrix products: 67.5 us -> none  [the longest x1 35.9 us: per_device(): lax.dot_general(grad_pre, cand_rows, (((0,), (0,)), ((), ())), preferred_...]
    psum x2 -> x0, blocking collectives: 56.6 us -> none  [the longest x1 44.2 us: per_device(): summed = lax.psum(owned, 'grp')]
    reduce_scatter x1 -> x0, waiting for transfers between devices: 51.3 us -> none  [per_device(): lax.psum_scatter(lax.dot_general(grad_pre, cand_rows, (((0,), (0,)), ((),...]
    all_gather x3 -> x0, blocking collectives: 29.4 us -> none  [the longest x1 10.7 us: per_device(): lax.all_gather(gain_vals, 'cand', axis=1, tiled=True)]
    all_gather x1 -> x0, waiting for transfers between devices: 18.5 us -> none  [per_device(): lax.all_gather(hidden_weight, 'cand', axis=0, tiled=True)]
    reduce_sum x2 -> x1, other arithmetic: 12 us -> 1.28 us  [per_device_fused(): scale = lax.rsqrt(jnp.sum(squares) / (hidden * width) + EPS)]
  transfers between devices with their start and end apart: 2 -> 0, of which waited for: 2 -> 0; matrix products, arithmetic and copies ran while one was open for 1% -> 0% of each run, Pallas kernels for 0% -> 0%
where the time goes in v1:
time: 123 us; the launch traced here: 122 us
  Pallas kernels  112 us (91%)
  other arithmetic  6.11 us (5%)
  local copies, waits for them, and re-layouts  3.32 us (3%)
  between operations  1.34 us (1%)
    pallas_call x1, Pallas kernels, per_device_fused(): pl.pallas_call(functools.partial(step_kernel, groups), out_shape=(jax.Sha...  112 us

profile of v1, /device:TPU:0, one launch (start us, length us, event | category | flops | bytes accessed | tf_op | source)
XLA Modules:
  0.0 122.4 jit_solution(10090645575848456693)
XLA Ops:
  0.6 0.7 broadcast_divide_fusion
  1.3 0.7 reshape.16
  2.0 0.7 broadcast_in_dim.2.hinv_ref
  2.7 0.7 divide_bitcast_fusion
  3.4 0.6 pad_maximum_fusion.gd_ref
  4.0 1.3 %copy.8.sw_ref = f32[2048,1]{1,0:T(8,128)} copy(f32[2048,1]{0,1:T(1,128)S(1)} %bitcast.7) | data formatting | bytes 16384 | tf_op jit(solution)/shard_map/reshape | solution.py:498
  5.3 111.6 %shard_map.77 = (bf16[256,1024]{1,0:T(8,128)(2,1)}, f32[8,128]{1,0:T(8,128)}, f32[24,128]{1,0:T(8,128)}) custom-call(bf16[3072,1024]{1,0:T(8,128)(2,1)} %bitcast.6, bf16[256,1024]{1,0:T(8,128)(2,1)} %w_hbm.1, f32[2048,1]{1,0:T(8,128)} %copy.8.sw_ref, f32[2,24,128]{2,1,0:T(8,128)} %pad_maximum_fusion.gd_ref, f32[24,128]{1,0:T(8,128)} %broadcast_in_dim.2.hinv_ref), custom_call_target="tpu_custom_call" | custom-call | tf_op jit(solution)/shard_map/pallas_call | solution.py:443
  117.0 1.3 %reduce_sum.9 = f32[]{:T(128)} reduce(f32[8,128]{1,0:T(8,128)} %get-tuple-element.6, f32[]{:T(128)} %constant.16.clone.1), dimensions={0,1}, to_apply=%region_0.0 | reduce | flops 1023 | bytes 4104 | tf_op jit(solution)/shard_map/reduce_sum | solution.py:502
  119.0 2.1 %convert_multiply_fusion = f32[256,1024]{1,0:T(8,128)} fusion(bf16[256,1024]{1,0:T(8,128)(2,1)} %get-tuple-element.5, f32[]{:T(128)S(6)} %rsqrt.3), kind=kLoop, calls=%fused_computation | loop fusion | flops 524288 | bytes 1572868 | tf_op jit(solution)/shard_map/mul | solution.py:503
  121.1 1.3 %copy.10 = f32[24,128]{1,0:T(8,128)} copy(f32[24,128]{1,0:T(8,128)} %get-tuple-element.13) | data formatting | bytes 24576
